TPU v7x, 256 devices: a whole 4x4x8 slice. The times are simulated.
256 devices in a mesh: cache: 32 (over x, z), owner: 8 (over y, core).
Axes of the slice: x: 4, y: 4, z: 8, core: 2. Of those that a mesh axis runs over, the one named last changes fastest.
Arguments:
- cache: bfloat16 [32, 4, 128, 256], P('cache'), may hold values from -2.5 to 2.5
- backing: bfloat16 [32, 64, 128, 256], P('cache', 'owner'), may hold values from -2.5 to 2.5
- resident: int32 [32, 4], P('cache'), may hold values from 0 to 63, as said below
- promote: int32 [32, 2], P('cache'), may hold values from 0 to 63, as said below
- victim: int32 [32, 2], P('cache'), may hold values from 0 to 3, as said below
- lookups: int32 [2, 32768, 32, 8], P(None, 'owner', 'cache'), may hold values from 0 to 511
- route: int32 [2, 8, 4096], P(None, 'owner'), may hold values from 0 to 4095, each once within a row
- dcn_down: bfloat16 [8192, 128], P('cache'), may hold values from -0.0625 to 0.0625
- dcn_up: bfloat16 [128, 8192], P(None, 'cache'), may hold values from -0.5 to 0.5
- dcn_bias: float32 [8192], replicated, may hold values from -5 to 5
- mlp_in: bfloat16 [8192, 1024], P('cache'), may hold values from -0.0625 to 0.0625
- mlp_bias: float32 [1024], replicated, may hold values from -3 to 3
- mlp_out: float32 [1024], replicated, may hold values from -0.1875 to 0.1875
- out_bias: float32 [1], replicated, may hold values from -4 to 4
Outputs:
- scores: float32 [2, 8, 4096], P(None, 'owner', 'cache')
- new_cache: bfloat16 [32, 4, 128, 256], P('cache')
- new_backing: bfloat16 [32, 64, 128, 256], P('cache', 'owner')
Inputs may be any that keep to these rules, and one draw needn't show every extreme that they name: `resident`: for each feature, 4 distinct backing blocks. `promote`: for each feature, 2 distinct backing blocks, none of them in that feature's resident; block k belongs to owner k // 8. `victim`: for each feature, 2 distinct slots. `route`: each batch and owner group holds every request index once.
All inputs are finite; a program needn't handle non-finite values.
Results may differ from a plain program's by a relative error of at most 0.004.
Values may be sent and summed in bfloat16 or wider, within the bound.
No kernel may reach another device: no remote copies, remote signals or barrier semaphores. Data moves between devices by JAX's collectives and lax.ppermute only.
A program may use at most 128 MiB of HBM per device.

v0:
```python
import jax
import jax.numpy as jnp
from jax import lax
from jax.sharding import PartitionSpec as P


def copy_for_each(x, axis):
    size = lax.axis_size(axis)
    return lax.all_to_all(jnp.broadcast_to(x[None], (size, *x.shape)), axis, 0, 0, tiled=True)


def in_order(blocks, dim):
    lengths = list(blocks.shape[1:])
    lengths[dim] *= blocks.shape[0]
    return jnp.moveaxis(blocks, 0, dim).reshape(lengths)


def gathered_copies(x, axis, dim):
    blocks = copy_for_each(x, axis)
    return in_order(blocks, dim)


def take_rows(table, wanted):
    return jax.vmap(lambda rows, chosen: rows[chosen])(table, wanted)


def pool_batch(requests, order, table):
    requests = requests[order]
    count = requests.shape[0]
    step = min(512, count)
    codes = jnp.arange(table.shape[1], dtype=jnp.int32)

    def one_block(lookup_block):
        counts = jnp.sum((lookup_block[..., None] == codes).astype(jnp.bfloat16), axis=2)
        return jnp.einsum("rfk,fke->rfe", counts, table, preferred_element_type=jnp.float32).astype(
            jnp.bfloat16
        )

    blocks = requests.reshape((count // step, step) + requests.shape[1:])
    pooled = lax.map(one_block, blocks)
    return pooled.reshape((count,) + pooled.shape[2:])


def on_device(
    cache,
    backing,
    resident,
    promote,
    victim,
    lookups,
    route,
    dcn_down,
    dcn_up,
    dcn_bias,
    mlp_in,
    mlp_bias,
    mlp_out,
    out_bias,
):
    held = cache.shape[0]
    slots = cache.shape[1]
    block = cache.shape[2]
    width = cache.shape[3]
    own_blocks = backing.shape[1]
    promoted_count = promote.shape[1]
    owner_here = lax.axis_index("owner")
    local_index = promote - owner_here * own_blocks
    owned_here = (local_index >= 0) & (local_index < own_blocks)
    clamped = jnp.clip(local_index, 0, own_blocks - 1)
    fetched = take_rows(backing, clamped)
    outgoing = jnp.where(owned_here[:, :, None, None], fetched, jnp.zeros_like(fetched))
    arrived = gathered_copies(outgoing, "owner", 0)
    owners = arrived.shape[0] // held
    arrived = arrived.reshape(owners, held, promoted_count, block, width)
    source = promote // own_blocks
    picked = source[None] == jnp.arange(owners, dtype=jnp.int32)[:, None, None]
    promoted = jnp.sum(jnp.where(picked[..., None, None], arrived, jnp.zeros_like(arrived)), axis=0)
    evicted = take_rows(cache, victim)
    leaving = take_rows(resident, victim) - owner_here * own_blocks
    slot_numbers = jnp.arange(slots, dtype=jnp.int32)
    block_numbers = jnp.arange(own_blocks, dtype=jnp.int32)
    new_cache = cache
    new_backing = backing
    for column in range(promoted_count):
        slot_hit = victim[:, column][:, None] == slot_numbers[None, :]
        new_cache = jnp.where(slot_hit[:, :, None, None], promoted[:, column][:, None], new_cache)
        block_hit = leaving[:, column][:, None] == block_numbers[None, :]
        new_backing = jnp.where(
            block_hit[:, :, None, None], evicted[:, column][:, None], new_backing
        )
    table = new_cache.reshape(held, slots * block, width)
    batches = lookups.shape[0]
    received = []
    for batch_turn in range(batches):
        pooled = pool_batch(lookups[batch_turn], route[batch_turn, 0], table)
        received.append(lax.all_to_all(pooled, "cache", split_axis=0, concat_axis=1, tiled=True))
    arrived_rows = jnp.stack(received)
    per_batch = arrived_rows.shape[1]
    features = arrived_rows.reshape(batches * per_batch, -1)
    columns = features
    low = jnp.dot(
        columns,
        lax.all_gather(dcn_down, "cache", axis=0, tiled=True),
        preferred_element_type=jnp.float32,
    ).astype(jnp.bfloat16)
    gate = (
        jnp.dot(
            low,
            lax.all_gather(dcn_up, "cache", axis=1, tiled=True),
            preferred_element_type=jnp.float32,
        )
        + dcn_bias
    )
    crossed = (features * gate + features).astype(jnp.bfloat16)
    columns = crossed
    before = jnp.dot(
        columns,
        lax.all_gather(mlp_in, "cache", axis=0, tiled=True),
        preferred_element_type=jnp.float32,
    )
    hidden = jnp.maximum(before + mlp_bias, 0.0)
    scores = jnp.sum(hidden * mlp_out, axis=-1) + out_bias[0]
    return (scores.reshape(batches, 1, per_batch), new_cache, new_backing)


def solution(mesh):
    in_specs = (
        P("cache", None, None, None),
        P("cache", "owner", None, None),
        P("cache", None),
        P("cache", None),
        P("cache", None),
        P(None, "owner", "cache", None),
        P(None, "owner", None),
        P("cache", None),
        P(None, "cache"),
        P(),
        P("cache", None),
        P(),
        P(),
        P(),
    )
    out_specs = (
        P(None, "owner", "cache"),
        P("cache", None, None, None),
        P("cache", "owner", None, None),
    )
    return jax.shard_map(
        on_device, mesh=mesh, in_specs=in_specs, out_specs=out_specs, check_vma=False
    )
```

profile of v0, /device:TPU:1, one launch (start us, length us, event | category | flops | bytes accessed | tf_op | source)
XLA Modules:
  0.0 363.3 jit_solution(7484960167387886002)
XLA Ops:
  13.9 6.7 %all-to-all-start = ((bf16[8,1,2,128,256]{4,3,2,1,0:T(8,128)(2,1)}), bf16[8,1,2,128,256]{4,3,2,1,0:T(8,128)(2,1)S(1)}, u32[]{:S(2)}, u32[]{:S(2)}) async-start(bf16[8,1,2,128,256]{4,3,2,1,0:T(8,128)(2,1)} %broadcast_in_dim.137), calls=%async_computation | async-start | bytes 2097152 | tf_op jit(solution)/shard_map/all_to_all | solution.py:9
  21.2 14.1 %gather_fusion = s32[4096,8]{1,0:T(8,128)} fusion(s32[4096,8]{1,0:T(8,128)S(1)} %bitcast.111, s32[4096]{0:T(1024)S(1)} %broadcast_clamp_fusion.1), kind=kCustom, calls=%fused_computation | custom fusion | bytes 278528 | tf_op jit(solution)/shard_map/gather | solution.py:28
  38.8 14.1 %gather_fusion.1 = s32[4096,8]{1,0:T(8,128)} fusion(s32[4096,8]{1,0:T(8,128)S(1)} %bitcast.110, s32[4096]{0:T(1024)S(1)} %broadcast_clamp_fusion), kind=kCustom, calls=%fused_computation.1 | custom fusion | bytes 278528 | tf_op jit(solution)/shard_map/gather | solution.py:28
  57.6 35.3 %while.26 = (s32[]{:T(128)}, bf16[8,512,1,256]{3,1,2,0:T(8,128)(2,1)S(1)}, s32[8,512,1,8]{1,3,2,0:T(8,128)}, bf16[1,512,256]{2,1,0:T(8,128)(2,1)S(1)}, s32[]{:T(128)}) while((s32[]{:T(128)}, bf16[8,512,1,256]{3,1,2,0:T(8,128)(2,1)S(1)}, s32[8,512,1,8]{1,3,2,0:T(8,128)}, bf16[1,512,256]{2,1,0:T(8,128)(2,1)S(1)}, s32[]{:T(128)}) %tuple.90), condition=%wide.region_3.4_spmd.clone, body=%wide.region_1.3_spmd.clone.sunk | while | flops 140378112 | bytes 1654853 | solution.py:40
  58.4 3.2 fusion.41
  62.8 3.2 fusion.41
  67.2 3.2 fusion.41
  76.1 3.2 fusion.41
  80.5 3.2 fusion.41
  84.9 3.2 fusion.41
  96.3 4.0 %reshape.321 = bf16[32,2,16384]{2,1,0:T(2,128)(2,1)} reshape(bf16[4096,256]{1,0:T(8,128)(2,1)} %reduce.17) | data formatting | bytes 4194304
  100.3 10.3 %all-to-all-start.1 = ((bf16[32,2,16384]{2,1,0:T(2,128)(2,1)}), bf16[32,2,16384]{2,1,0:T(2,128)(2,1)S(1)}, u32[]{:S(2)}, u32[]{:S(2)}) async-start(bf16[32,2,16384]{2,1,0:T(2,128)(2,1)} %reshape.321), calls=%async_computation.1 | async-start | bytes 4194304 | tf_op jit(solution)/shard_map/all_to_all | solution.py:96
  112.1 35.1 %while.27 = (s32[]{:T(128)}, bf16[8,512,1,256]{3,1,2,0:T(8,128)(2,1)}, s32[8,512,1,8]{1,3,2,0:T(8,128)S(1)}, bf16[1,512,256]{2,1,0:T(8,128)(2,1)S(1)}, s32[]{:T(128)}) while((s32[]{:T(128)}, bf16[8,512,1,256]{3,1,2,0:T(8,128)(2,1)}, s32[8,512,1,8]{1,3,2,0:T(8,128)S(1)}, bf16[1,512,256]{2,1,0:T(8,128)(2,1)S(1)}, s32[]{:T(128)}) %tuple.91), condition=%wide.region_6.7_spmd.clone, body=%wide.region_4.6_spmd.clone.sunk | while | flops 140378112 | bytes 1655361 | solution.py:40
  147.2 4.5 %reduce.16 = bf16[4096,256]{1,0:T(8,128)(2,1)} reduce(bf16[4096,1,256]{2,0,1:T(8,128)(2,1)} %bitcast.116, bf16[]{:T(256)} %broadcast.259), dimensions={1}, to_apply=%copy.68.reduce_sub_computation | reduce | bytes 4194306 | tf_op jit(solution)/shard_map/reshape | solution.py:41
  151.7 4.0 %reshape.319 = bf16[32,2,16384]{2,1,0:T(2,128)(2,1)} reshape(bf16[4096,256]{1,0:T(8,128)(2,1)} %reduce.16) | data formatting | bytes 4194304
  155.7 6.3 %all-to-all-done.1 = bf16[32,2,16384]{2,1,0:T(2,128)(2,1)S(1)} async-done(((bf16[32,2,16384]{2,1,0:T(2,128)(2,1)}), bf16[32,2,16384]{2,1,0:T(2,128)(2,1)S(1)}, u32[]{:S(2)}, u32[]{:S(2)}) %all-to-all-start.1) | async-done | bytes 2097184 | tf_op jit(solution)/shard_map/all_to_all | solution.py:96
  162.0 10.4 %all-to-all-start.2 = ((bf16[32,2,16384]{2,1,0:T(2,128)(2,1)}), bf16[32,2,16384]{2,1,0:T(2,128)(2,1)}, u32[]{:S(2)}, u32[]{:S(2)}) async-start(bf16[32,2,16384]{2,1,0:T(2,128)(2,1)} %reshape.319), calls=%async_computation.2 | async-start | bytes 4194304 | tf_op jit(solution)/shard_map/all_to_all | solution.py:96
  177.5 6.7 %reshape.322 = bf16[4096,1,256]{2,1,0:T(2,128)(2,1)} reshape(bf16[32,2,16384]{2,1,0:T(2,128)(2,1)S(1)} %all-to-all-done.1) | data formatting | bytes 4194304
  186.8 41.1 %all-to-all-done.2 = bf16[32,2,16384]{2,1,0:T(2,128)(2,1)} async-done(((bf16[32,2,16384]{2,1,0:T(2,128)(2,1)}), bf16[32,2,16384]{2,1,0:T(2,128)(2,1)}, u32[]{:S(2)}, u32[]{:S(2)}) %all-to-all-start.2) | async-done | bytes 2097184 | tf_op jit(solution)/shard_map/all_to_all | solution.py:96
  227.9 10.4 %reshape.320 = bf16[4096,1,256]{2,1,0:T(2,128)(2,1)} reshape(bf16[32,2,16384]{2,1,0:T(2,128)(2,1)} %all-to-all-done.2) | data formatting | bytes 4194304
  243.7 6.2 %copy.77 = bf16[32,8,32,256]{3,1,2,0:T(8,128)(2,1)} copy(bf16[32,8,32,256]{3,2,1,0:T(8,128)(2,1)S(1)} %bitcast.114) | data formatting | bytes 8388608
  249.9 4.1 %convolution_convert_fusion.2 = bf16[256,128]{1,0:T(8,128)(2,1)S(1)} fusion(bf16[256,8192]{1,0:T(8,128)(2,1)} %bitcast.112, bf16[8192,128]{1,0:T(8,128)(2,1)} %all-gather.4.cloned.1.call-done), kind=kOutput, calls=%fused_computation.31 | convolution fusion | flops 536903680 | bytes 6356992 | tf_op jit(solution)/shard_map/dot_general | solution.py:101
  254.1 89.4 %all-gather.8.cloned.1.call-done = bf16[8192,1024]{1,0:T(8,128)(2,1)} async-done(((bf16[256,1024]{1,0:T(8,128)(2,1)}), bf16[8192,1024]{1,0:T(8,128)(2,1)}) %all-gather.8.cloned.1.call-update) | async-done | bytes 16777232 | tf_op jit(solution)/shard_map/all_gather | solution.py:118
  343.5 12.7 %fusion.17 = f32[256]{0:T(256)S(1)} fusion(bf16[8192,1024]{1,0:T(8,128)(2,1)} %all-gather.8.cloned.1.call-done, bf16[256,128]{1,0:T(8,128)(2,1)S(1)} %convolution_convert_fusion.2, bf16[128,8192]{1,0:T(8,128)(2,1)} %all-gather.6.cloned.1.call-done, bf16[256,8192]{1,0:T(8,128)(2,1)} %bitcast.113, f32[8192]{0:T(1024)S(1)} %copy-done.8, ...), kind=kOutput, calls=%fused_computation.30 | convolution fusion | flops 4843372544 | bytes 23176192 | tf_op jit(solution)/shard_map/dot_general | solution.py:116
  (131 shorter events, 83.8 us)
Async XLA Ops:
  7.2 166.8 %copy-start = (s32[1,4]{1,0:T(1,128)S(1)}, s32[1,4]{1,0:T(1,128)}, u32[]{:S(2)}) copy-start(s32[1,4]{1,0:T(1,128)} %param.20) | copy-start | bytes 52
  7.2 242.7 %all-gather.4.cloned.1.call-start = ((), (), s32[]{:S(2)}) async-start(), calls=%async_computation.3 | async-start | bytes 2162688 | tf_op jit(solution)/shard_map/all_gather | solution.py:103
  7.9 246.2 %all-gather.6.cloned.1.call-start = ((), (), s32[]{:S(2)}) async-start(), calls=%async_computation.4 | async-start | bytes 2162688 | tf_op jit(solution)/shard_map/all_gather | solution.py:109
  8.7 11.9 %copy-start.5 = (s32[2,4096,1,8]{1,3,2,0:T(8,128)S(1)}, s32[2,4096,1,8]{1,3,2,0:T(8,128)}, u32[]{:S(2)}) copy-start(s32[2,4096,1,8]{1,3,2,0:T(8,128)} %param.23) | copy-start | bytes 786436
  8.7 334.8 %all-gather.8.cloned.1.call-start = ((), (), s32[]{:S(2)}) async-start(), calls=%async_computation.5 | async-start | bytes 17301504 | tf_op jit(solution)/shard_map/all_gather | solution.py:118
  12.0 8.5 %copy-start.6 = (s32[2,1,4096]{2,1,0:T(1,128)S(1)}, s32[2,1,4096]{2,1,0:T(1,128)}, u32[]{:S(2)}) copy-start(s32[2,1,4096]{2,1,0:T(1,128)} %param.24) | copy-start | bytes 98308
  13.9 43.2 %all-to-all-start = ((bf16[8,1,2,128,256]{4,3,2,1,0:T(8,128)(2,1)}), bf16[8,1,2,128,256]{4,3,2,1,0:T(8,128)(2,1)S(1)}, u32[]{:S(2)}, u32[]{:S(2)}) async-start(bf16[8,1,2,128,256]{4,3,2,1,0:T(8,128)(2,1)} %broadcast_in_dim.137), calls=%async_computation | async-start | bytes 2097152 | tf_op jit(solution)/shard_map/all_to_all | solution.py:9
  52.9 2.2 copy-start.7
  52.9 4.4 %copy-start.3 = (bf16[1,4,128,256]{3,2,1,0:T(8,128)(2,1)S(1)}, bf16[1,4,128,256]{3,2,1,0:T(8,128)(2,1)}, u32[]{:S(2)}) copy-start(bf16[1,4,128,256]{3,2,1,0:T(8,128)(2,1)} %param.18) | copy-start | bytes 786436
  100.3 61.7 %all-to-all-start.1 = ((bf16[32,2,16384]{2,1,0:T(2,128)(2,1)}), bf16[32,2,16384]{2,1,0:T(2,128)(2,1)S(1)}, u32[]{:S(2)}, u32[]{:S(2)}) async-start(bf16[32,2,16384]{2,1,0:T(2,128)(2,1)} %reshape.321), calls=%async_computation.1 | async-start | bytes 4194304 | tf_op jit(solution)/shard_map/all_to_all | solution.py:96
  147.2 4.5 %copy-start.4 = (bf16[1,512,256]{2,1,0:T(8,128)(2,1)}, bf16[1,512,256]{2,1,0:T(8,128)(2,1)S(1)}, u32[]{:S(2)}) copy-start(bf16[1,512,256]{2,1,0:T(8,128)(2,1)S(1)} %get-tuple-element.330) | copy-start | bytes 786436
  155.7 20.8 %copy-start.2 = (bf16[1,8,128,256]{3,2,1,0:T(8,128)(2,1)S(1)}, bf16[1,8,128,256]{3,2,1,0:T(8,128)(2,1)}, u32[]{:S(2)}) copy-start(bf16[1,8,128,256]{3,2,1,0:T(8,128)(2,1)} %param.19) | copy-start | bytes 1572868
  162.0 65.9 %all-to-all-start.2 = ((bf16[32,2,16384]{2,1,0:T(2,128)(2,1)}), bf16[32,2,16384]{2,1,0:T(2,128)(2,1)}, u32[]{:S(2)}, u32[]{:S(2)}) async-start(bf16[32,2,16384]{2,1,0:T(2,128)(2,1)} %reshape.319), calls=%async_computation.2 | async-start | bytes 4194304 | tf_op jit(solution)/shard_map/all_to_all | solution.py:96
  249.9 93.6 %copy-start.8 = (f32[8192]{0:T(1024)S(1)}, f32[8192]{0:T(1024)}, u32[]{:S(2)}) copy-start(f32[8192]{0:T(1024)} %param.27) | copy-start | bytes 98308
  249.9 93.6 %copy-start.9 = (f32[1024]{0:T(1024)S(1)}, f32[1024]{0:T(1024)}, u32[]{:S(2)}) copy-start(f32[1024]{0:T(1024)} %param.30) | copy-start | bytes 12292
  249.9 93.6 %copy-start.10 = (f32[1024]{0:T(1024)S(1)}, f32[1024]{0:T(1024)}, u32[]{:S(2)}) copy-start(f32[1024]{0:T(1024)} %param.29) | copy-start | bytes 12292
  343.5 13.2 %copy-start.1 = (s32[1,4]{1,0:T(1,128)S(1)}, s32[1,4]{1,0:T(1,128)}, u32[]{:S(2)}) copy-start(s32[1,4]{1,0:T(1,128)} %param.20) | copy-start | bytes 52
Sparse Core Ops, SparseCore 0:
  10.6 77.0 all-gather.3
  90.1 95.1 all-gather.5
  187.9 155.6 all-gather.7
where the time goes:
time: 365 us; the launch traced here: 363 us
  waiting for transfers between devices  139 us (38%)
  local copies, waits for them, and re-layouts  88.8 us (24%)
  other arithmetic  65.7 us (18%)
  starting transfers between devices  27.5 us (8%)
  matrix products  27.3 us (7%)
  between operations  14.7 us (4%)
    all_gather x1, waiting for transfers between devices, on_device(): lax.all_gather(mlp_in, 'cache', axis=0, tiled=True)  89.4 us
    reduce_sum x16, other arithmetic, one_block(): jnp.sum((lookup_block[..., None] == codes).astype(jnp.bfloat16), axis=2)  51.7 us
    all_to_all x2, waiting for transfers between devices, on_device(): lax.all_to_all(pooled, 'cache', split_axis=0, concat_axis=1, tiled=True)  47.4 us
    unnamed x35, local copies, waits for them, and re-layouts  42.9 us
    gather x2, local copies, waits for them, and re-layouts, pool_batch(): requests = requests[order]  28.2 us
    all_to_all x2, starting transfers between devices, on_device(): lax.all_to_all(pooled, 'cache', split_axis=0, concat_axis=1, tiled=True)  20.7 us
    dot_general x1, matrix products, on_device(): jnp.dot(columns, lax.all_gather(mlp_in, 'cache', axis=0, tiled=True), pre...  12.7 us
    dot_general x16, matrix products, one_block(): jnp.einsum('rfk,fke->rfe', counts, table, preferred_element_type=jnp.floa...  10.5 us
  transfers between devices with their start and end apart: 6, of which 3 were waited for; matrix products, arithmetic and copies ran while one was open for 46% of the time, Pallas kernels for 0%

commit v1 on v0

--- a/solution.py
+++ b/solution.py
@@ -2,6 +2,13 @@
 import jax.numpy as jnp
 from jax import lax
 from jax.sharding import PartitionSpec as P
+
+
+def swapped_in(x, axis, dim):
+    size = lax.axis_size(axis)
+    blocks = jnp.stack([x for _ in range(size)])
+    blocks = lax.all_to_all(blocks, axis, split_axis=0, concat_axis=0)
+    return jnp.concatenate(blocks, axis=dim)
 
 
 def copy_for_each(x, axis):
@@ -113,11 +120,7 @@
     )
     crossed = (features * gate + features).astype(jnp.bfloat16)
     columns = crossed
-    before = jnp.dot(
-        columns,
-        lax.all_gather(mlp_in, "cache", axis=0, tiled=True),
-        preferred_element_type=jnp.float32,
-    )
+    before = jnp.dot(columns, swapped_in(mlp_in, "cache", 0), preferred_element_type=jnp.float32)
     hidden = jnp.maximum(before + mlp_bias, 0.0)
     scores = jnp.sum(hidden * mlp_out, axis=-1) + out_bias[0]
     return (scores.reshape(batches, 1, per_batch), new_cache, new_backing)

time: 365 us -> 675 us (1.85)
  the two profiles are of different devices: /device:TPU:1 before, /device:TPU:163 now
where the time goes in v1:
time: 675 us; the launch traced here: 674 us
  waiting for transfers between devices  393 us (58%)
  local copies, waits for them, and re-layouts  93.1 us (14%)
  other arithmetic  65.8 us (10%)
  blocking collectives  56.7 us (8%)
  matrix products  27.3 us (4%)
  starting transfers between devices  22.8 us (3%)
  between operations  14.9 us (2%)
    all_gather x1, waiting for transfers between devices, on_device(): lax.all_gather(dcn_up, 'cache', axis=1, tiled=True)  300 us
    all_gather x1, waiting for transfers between devices, on_device(): lax.all_gather(dcn_down, 'cache', axis=0, tiled=True)  69.9 us
    all_to_all x1, blocking collectives, on_device(): lax.all_to_all(pooled, 'cache', split_axis=0, concat_axis=1, tiled=True)  56.7 us
    reduce_sum x16, other arithmetic, one_block(): jnp.sum((lookup_block[..., None] == codes).astype(jnp.bfloat16), axis=2)  51.7 us
    unnamed x39, local copies, waits for them, and re-layouts  41.3 us
    gather x2, local copies, waits for them, and re-layouts, pool_batch(): requests = requests[order]  28.4 us
    all_to_all x1, waiting for transfers between devices, swapped_in(): blocks = lax.all_to_all(blocks, axis, split_axis=0, concat_axis=0)  19.1 us
  transfers between devices with their start and end apart: 5, of which 4 were waited for; matrix products, arithmetic and copies ran while one was open for 18% of the time, Pallas kernels for 0%

profile of v1, /device:TPU:163, one launch (start us, length us, event | category | flops | bytes accessed | tf_op | source)
XLA Modules:
  0.0 674.0 jit_solution(6672117433344591302)
XLA Ops:
  11.7 5.1 all-to-all-start
  17.5 14.2 %gather_fusion.1 = s32[4096,8]{1,0:T(8,128)} fusion(s32[4096,8]{1,0:T(8,128)S(1)} %bitcast.112, s32[4096]{0:T(1024)S(1)} %broadcast_clamp_fusion), kind=kCustom, calls=%fused_computation.1 | custom fusion | bytes 278528 | tf_op jit(solution)/shard_map/gather | solution.py:35
  35.2 14.2 %gather_fusion = s32[4096,8]{1,0:T(8,128)} fusion(s32[4096,8]{1,0:T(8,128)S(1)} %bitcast.111, s32[4096]{0:T(1024)S(1)} %broadcast_clamp_fusion.1), kind=kCustom, calls=%fused_computation | custom fusion | bytes 278528 | tf_op jit(solution)/shard_map/gather | solution.py:35
  53.9 35.3 %while.27 = (s32[]{:T(128)}, bf16[8,512,1,256]{3,1,2,0:T(8,128)(2,1)S(1)}, s32[8,512,1,8]{1,3,2,0:T(8,128)}, bf16[1,512,256]{2,1,0:T(8,128)(2,1)S(1)}, s32[]{:T(128)}) while((s32[]{:T(128)}, bf16[8,512,1,256]{3,1,2,0:T(8,128)(2,1)S(1)}, s32[8,512,1,8]{1,3,2,0:T(8,128)}, bf16[1,512,256]{2,1,0:T(8,128)(2,1)S(1)}, s32[]{:T(128)}) %tuple.88), condition=%wide.region_6.7_spmd.clone, body=%wide.region_4.6_spmd.clone.sunk | while | flops 140378112 | bytes 1654861 | solution.py:47
  54.8 3.2 fusion.45
  59.2 3.2 fusion.45
  63.6 3.2 fusion.45
  92.7 4.0 reshape.325
  96.7 8.8 %all-to-all-start.2 = ((bf16[32,2,16384]{2,1,0:T(2,128)(2,1)}), bf16[32,2,16384]{2,1,0:T(2,128)(2,1)S(1)}, u32[]{:S(2)}, u32[]{:S(2)}) async-start(bf16[32,2,16384]{2,1,0:T(2,128)(2,1)} %reshape.325), calls=%async_computation.2 | async-start | bytes 4194304 | tf_op jit(solution)/shard_map/all_to_all | solution.py:103
  106.9 35.1 %while.26 = (s32[]{:T(128)}, bf16[8,512,1,256]{3,1,2,0:T(8,128)(2,1)}, s32[8,512,1,8]{1,3,2,0:T(8,128)S(1)}, bf16[1,512,256]{2,1,0:T(8,128)(2,1)S(1)}, s32[]{:T(128)}) while((s32[]{:T(128)}, bf16[8,512,1,256]{3,1,2,0:T(8,128)(2,1)}, s32[8,512,1,8]{1,3,2,0:T(8,128)S(1)}, bf16[1,512,256]{2,1,0:T(8,128)(2,1)S(1)}, s32[]{:T(128)}) %tuple.89), condition=%wide.region_3.4_spmd.clone, body=%wide.region_1.3_spmd.clone.sunk | while | flops 140378112 | bytes 1654861 | solution.py:47
  142.0 4.5 reduce.17
  146.5 4.0 reshape.327
  152.9 56.7 %all_to_all.40 = bf16[32,2,16384]{2,1,0:T(2,128)(2,1)} all-to-all(bf16[32,2,16384]{2,1,0:T(2,128)(2,1)} %reshape.327), channel_id=1, replica_groups=mesh['cache'=32,'owner'=8] {'cache'}, dimensions={0} | all-to-all | bytes 4194304 | tf_op jit(solution)/shard_map/all_to_all | solution.py:103
  209.6 5.9 stack.11
  215.6 8.6 %all-to-all-start.3 = ((bf16[32,256,1024]{2,1,0:T(8,128)(2,1)}), bf16[32,256,1024]{2,1,0:T(8,128)(2,1)}, u32[]{:S(2)}, u32[]{:S(2)}) async-start(bf16[32,256,1024]{2,1,0:T(8,128)(2,1)} %stack.11), calls=%async_computation.3 | async-start | bytes 33554432 | tf_op jit(solution)/shard_map/all_to_all | solution.py:10
  230.7 6.8 %reshape.326 = bf16[4096,1,256]{2,1,0:T(2,128)(2,1)} reshape(bf16[32,2,16384]{2,1,0:T(2,128)(2,1)S(1)} %all-to-all-done.2) | data formatting | bytes 4194304
  237.6 4.0 copy.72
  241.6 6.8 %reshape.328 = bf16[4096,1,256]{2,1,0:T(2,128)(2,1)} reshape(bf16[32,2,16384]{2,1,0:T(2,128)(2,1)S(1)} %copy-done.1) | data formatting | bytes 4194304
  254.1 6.4 copy.77
  260.4 69.9 %all-gather.3.cloned.1.call-done = bf16[8192,128]{1,0:T(8,128)(2,1)} async-done(((bf16[256,128]{1,0:T(8,128)(2,1)}), bf16[8192,128]{1,0:T(8,128)(2,1)}) %all-gather.3.cloned.1.call-update) | async-done | bytes 2097168 | tf_op jit(solution)/shard_map/all_gather | solution.py:110
  330.3 4.1 convolution_convert_fusion.2
  334.5 300.4 %all-gather.5.cloned.1.call-done = bf16[128,8192]{1,0:T(8,128)(2,1)} async-done(((bf16[128,256]{1,0:T(8,128)(2,1)}), bf16[128,8192]{1,0:T(8,128)(2,1)}) %all-gather.5.cloned.1.call-update) | async-done | bytes 2097168 | tf_op jit(solution)/shard_map/all_gather | solution.py:116
  634.9 19.1 %all-to-all-done.3 = bf16[32,256,1024]{2,1,0:T(8,128)(2,1)} async-done(((bf16[32,256,1024]{2,1,0:T(8,128)(2,1)}), bf16[32,256,1024]{2,1,0:T(8,128)(2,1)}, u32[]{:S(2)}, u32[]{:S(2)}) %all-to-all-start.3) | async-done | bytes 16777248 | tf_op jit(solution)/shard_map/all_to_all | solution.py:10
  653.9 12.7 %fusion.17 = f32[256]{0:T(256)S(1)} fusion(bf16[8192,1024]{1,0:T(8,128)(2,1)} %bitcast.24, bf16[256,128]{1,0:T(8,128)(2,1)S(1)} %convolution_convert_fusion.2, bf16[128,8192]{1,0:T(8,128)(2,1)} %all-gather.5.cloned.1.call-done, bf16[256,8192]{1,0:T(8,128)(2,1)} %bitcast.114, f32[8192]{0:T(1024)S(1)} %copy-done.10, f32[1024]{0:T(1024)S(1)} %copy-done.11, ...), kind=kOutput, calls=%fused_computation.30 | convolution fusion | flops 4843372544 | bytes 23176192 | tf_op jit(solution)/shard_map/dot_general | solution.py:123
  (134 shorter events, 92.9 us)
Async XLA Ops:
  7.2 220.1 %copy-start = (s32[1,4]{1,0:T(1,128)S(1)}, s32[1,4]{1,0:T(1,128)}, u32[]{:S(2)}) copy-start(s32[1,4]{1,0:T(1,128)} %param.20) | copy-start | bytes 52
  7.2 9.7 %copy-start.7 = (s32[2,4096,1,8]{1,3,2,0:T(8,128)S(1)}, s32[2,4096,1,8]{1,3,2,0:T(8,128)}, u32[]{:S(2)}) copy-start(s32[2,4096,1,8]{1,3,2,0:T(8,128)} %param.23) | copy-start | bytes 786436
  10.5 6.3 copy-start.8
  11.7 41.7 %all-to-all-start = ((bf16[8,1,2,128,256]{4,3,2,1,0:T(8,128)(2,1)}), bf16[8,1,2,128,256]{4,3,2,1,0:T(8,128)(2,1)S(1)}, u32[]{:S(2)}, u32[]{:S(2)}) async-start(bf16[8,1,2,128,256]{4,3,2,1,0:T(8,128)(2,1)} %broadcast_in_dim.137), calls=%async_computation | async-start | bytes 2097152 | tf_op jit(solution)/shard_map/all_to_all | solution.py:16
  49.3 2.2 copy-start.9
  49.3 4.3 copy-start.4
  96.7 56.2 %all-to-all-start.2 = ((bf16[32,2,16384]{2,1,0:T(2,128)(2,1)}), bf16[32,2,16384]{2,1,0:T(2,128)(2,1)S(1)}, u32[]{:S(2)}, u32[]{:S(2)}) async-start(bf16[32,2,16384]{2,1,0:T(2,128)(2,1)} %reshape.325), calls=%async_computation.2 | async-start | bytes 4194304 | tf_op jit(solution)/shard_map/all_to_all | solution.py:103
  142.0 4.5 copy-start.6
  150.5 59.1 %copy-start.5 = (bf16[256,1024]{1,0:T(8,128)(2,1)S(1)}, bf16[256,1024]{1,0:T(8,128)(2,1)}, u32[]{:S(2)}) copy-start(bf16[256,1024]{1,0:T(8,128)(2,1)} %param.28) | copy-start | bytes 1572868
  215.6 14.2 %copy-start.3 = (bf16[1,8,128,256]{3,2,1,0:T(8,128)(2,1)S(1)}, bf16[1,8,128,256]{3,2,1,0:T(8,128)(2,1)}, u32[]{:S(2)}) copy-start(bf16[1,8,128,256]{3,2,1,0:T(8,128)(2,1)} %param.19) | copy-start | bytes 1572868
  215.6 438.3 %all-to-all-start.3 = ((bf16[32,256,1024]{2,1,0:T(8,128)(2,1)}), bf16[32,256,1024]{2,1,0:T(8,128)(2,1)}, u32[]{:S(2)}, u32[]{:S(2)}) async-start(bf16[32,256,1024]{2,1,0:T(8,128)(2,1)} %stack.11), calls=%async_computation.3 | async-start | bytes 33554432 | tf_op jit(solution)/shard_map/all_to_all | solution.py:10
  224.2 106.2 %all-gather.3.cloned.1.call-start = ((), (), s32[]{:S(2)}) async-start(), calls=%async_computation.4 | async-start | bytes 2162688 | tf_op jit(solution)/shard_map/all_gather | solution.py:110
  224.9 410.0 %all-gather.5.cloned.1.call-start = ((), (), s32[]{:S(2)}) async-start(), calls=%async_computation.5 | async-start | bytes 2162688 | tf_op jit(solution)/shard_map/all_gather | solution.py:116
  237.6 4.0 copy-start.1
  248.4 2.9 copy-start.2
  330.3 323.6 %copy-start.10 = (f32[8192]{0:T(1024)S(1)}, f32[8192]{0:T(1024)}, u32[]{:S(2)}) copy-start(f32[8192]{0:T(1024)} %param.27) | copy-start | bytes 98308
  330.3 323.6 %copy-start.11 = (f32[1024]{0:T(1024)S(1)}, f32[1024]{0:T(1024)}, u32[]{:S(2)}) copy-start(f32[1024]{0:T(1024)} %param.30) | copy-start | bytes 12292
  330.3 323.6 %copy-start.12 = (f32[1024]{0:T(1024)S(1)}, f32[1024]{0:T(1024)}, u32[]{:S(2)}) copy-start(f32[1024]{0:T(1024)} %param.29) | copy-start | bytes 12292
Sparse Core Ops, SparseCore 0:
  227.6 102.7 all-gather.2
  332.8 302.0 all-gather.4
